TPU v7x, 32 devices: a whole 2x2x4 slice. The times are simulated.
32 devices in a mesh: section: 8 (over z, x), expert: 4 (over y, core).
Axes of the slice: x: 2, y: 2, z: 4, core: 2. Of those that a mesh axis runs over, the one named last changes fastest.
Arguments:
- tokens: bfloat16 [16, 32, 768], P(None, 'expert'), may hold values from -6 to 6
- route_ids: int32 [8, 16, 32, 2], P('section'), may hold values from 0 to 3, all different within a row; in each aligned block of 8 rows (0 to 7, 8 to 15, ..., all dimensions but the last counted through in order) at most 8 rows name the same one
- router: bfloat16 [8, 768, 4], P('section'), may hold values from -0.21875 to 0.21875
- norm_gain: float32 [8, 768], P('section'), may hold values from 0.1 to 1.9
- weight_in: bfloat16 [8, 4, 768, 3072], P('section', 'expert'), may hold values from -0.21875 to 0.21875
- weight_out: bfloat16 [8, 4, 3072, 768], P('section', 'expert'), may hold values from -0.109375 to 0.109375
Outputs:
- layer_states: bfloat16 [8, 16, 32, 768], P('section', None, 'expert')
Inputs may be any that keep to these rules, and one draw needn't show every extreme that they name: `route_ids`: each row names two different experts. In each aligned block of 8 rows (the tokens of one micro-batch on one index of the expert axis) no expert is named by more than 8 rows, and in some blocks one expert is named by exactly 8.
All inputs are finite; a program needn't handle non-finite values.
Results may differ from a plain program's by a relative error of at most 0.028.
Values may be sent and summed in bfloat16 or wider, within the bound.
No kernel may reach another device: no remote copies, remote signals or barrier semaphores. Data moves between devices by JAX's collectives and lax.ppermute only.
A program may use at most 64 MiB of HBM per device.

v0:
```python
import jax
import jax.numpy as jnp
from jax import lax
from jax.sharding import PartitionSpec as P

epsilon = 1e-06


def from_behind(block, axis, distance):
    devices = range(lax.axis_size(axis))
    route = [(i - distance, i) for i in devices if i - distance in devices]
    return lax.ppermute(block, axis, route)


def slot_targets(route_block, experts, capacity):
    owners = route_block.shape[0]
    assigned = route_block.reshape(owners, -1)
    onehot = (assigned[:, :, None] == jnp.arange(experts, dtype=jnp.int32)[None, None, :]).astype(
        jnp.int32
    )
    earlier = jnp.cumsum(onehot, axis=1) - onehot
    position = jnp.sum(onehot * earlier, axis=2)
    return (assigned * capacity + position).reshape(route_block.shape)


def body(tokens, route_ids, router, norm_gain, weight_in, weight_out):
    groups = lax.axis_size("expert")
    sections = lax.axis_size("section")
    section_index = lax.axis_index("section")
    member = lax.axis_index("expert")
    micro_count, tok_rows, features = tokens.shape
    experts = router.shape[2]
    capacity = 4 * tok_rows // experts
    slot_total = experts * capacity
    routes_all = route_ids[0]
    router_block = router[0]
    gain_row = norm_gain[0]
    expert_in = weight_in[0, 0]
    expert_out = weight_out[0, 0]
    columns = jnp.arange(slot_total, dtype=jnp.int32)
    expert_range = jnp.arange(experts, dtype=jnp.int32)
    contract_rows = (((0,), (0,)), ((), ()))

    def apply_expert(received):
        flattened = received.reshape(-1, features)
        hidden = jax.nn.relu(
            jnp.dot(flattened, expert_in, preferred_element_type=jnp.float32)
        ).astype(jnp.bfloat16)
        produced = jnp.dot(hidden, expert_out, preferred_element_type=jnp.float32).astype(
            jnp.bfloat16
        )
        return lax.all_to_all(
            produced.reshape(received.shape), "expert", split_axis=0, concat_axis=0, tiled=True
        )

    def apply_layer(current, route_block):
        stream = current.astype(jnp.float32)
        inverse = lax.rsqrt(jnp.mean(stream * stream, axis=-1, keepdims=True) + epsilon)
        normed = (stream * inverse * gain_row).astype(jnp.bfloat16)
        logits = jnp.dot(normed, router_block, preferred_element_type=jnp.float32)
        owners_block = route_block.reshape(groups, tok_rows, 2)
        targets = slot_targets(owners_block, experts, capacity)
        own_targets = lax.dynamic_index_in_dim(targets, member, 0, keepdims=False)
        own_experts = lax.dynamic_index_in_dim(owners_block, member, 0, keepdims=False)
        selector = (own_targets[:, :, None] == columns[None, None, :]).astype(jnp.bfloat16)
        owner_base = jnp.arange(groups, dtype=jnp.int32)[:, None, None] * capacity
        place = jnp.where(owners_block == member, owner_base + targets - member * capacity, -1)
        receive_columns = jnp.arange(groups * capacity, dtype=jnp.int32)
        picker = jnp.sum(
            (place[..., None] == receive_columns[None, None, None, :]).astype(jnp.bfloat16), axis=2
        )
        picker = picker.reshape(groups * tok_rows, groups * capacity)
        collected = lax.dot_general(
            picker,
            lax.all_gather(normed, "expert", axis=0, tiled=True),
            contract_rows,
            preferred_element_type=jnp.float32,
        )
        returned = apply_expert(collected.astype(jnp.bfloat16).reshape(groups, capacity, features))
        picked = jnp.einsum(
            "tkr,rd->tkd",
            selector,
            returned.reshape(slot_total, features),
            preferred_element_type=jnp.float32,
        )
        chosen = (own_experts[:, :, None] == expert_range[None, None, :]).astype(jnp.float32)
        gate_values = jax.nn.sigmoid(jnp.sum(chosen * logits[:, None, :], axis=2))
        mixed = stream + gate_values[:, 0:1] * picked[:, 0] + gate_values[:, 1:2] * picked[:, 1]
        return mixed.astype(jnp.bfloat16)

    def relay_turn(counter, state_pair):
        received, states = state_pair
        offset_turn = counter - section_index
        active_turn = jnp.logical_and(offset_turn >= 0, offset_turn < micro_count)
        micro_index = jnp.clip(offset_turn, 0, micro_count - 1)
        entering = lax.dynamic_index_in_dim(tokens, micro_index, 0, keepdims=False)
        current = jnp.where(section_index == 0, entering, received)
        route_block = lax.dynamic_index_in_dim(routes_all, micro_index, 0, keepdims=False)
        result = apply_layer(current, route_block)
        previous = lax.dynamic_index_in_dim(states, micro_index, 0, keepdims=False)
        states = lax.dynamic_update_index_in_dim(
            states, jnp.where(active_turn, result, previous), micro_index, 0
        )
        received = from_behind(result, "section", 1)
        return (received, states)

    initial = (
        jnp.zeros((tok_rows, features), jnp.bfloat16),
        jnp.zeros((micro_count, tok_rows, features), jnp.bfloat16),
    )
    leftover, states = lax.fori_loop(0, micro_count + sections - 1, relay_turn, initial)
    return states[None]


def solution(mesh):
    placed = (
        P(None, "expert", None),
        P("section", None, None, None),
        P("section", None, None),
        P("section", None),
        P("section", "expert", None, None),
        P("section", "expert", None, None),
    )
    return jax.shard_map(
        body,
        mesh=mesh,
        in_specs=placed,
        out_specs=P("section", None, "expert", None),
        check_vma=False,
    )
```

profile of v0, /device:TPU:24, one launch (start us, length us, event | category | flops | bytes accessed | tf_op | source)
XLA Modules:
  0.0 645.4 jit_solution(5879649925889089358)
XLA Ops:
  0.9 643.8 %while.18 = (s32[]{:T(128)}, bf16[8,768]{1,0:T(8,128)(2,1)S(1)}, bf16[16,8,768]{2,1,0:T(8,128)(2,1)S(1)}, pred[]{:T(512)}, s32[]{:T(128)}, /*index=5*/bf16[16,8,...) while((s32[]{:T(128)}, bf16[8,768]{1,0:T(8,128)(2,1)S(1)}, ...), condition=%wide.region_6.7_spmd.clone, body=%wide.region_0.6_spmd.clone.sunk | while | flops 304748096 | bytes 10243028 | solution.py:111
  8.9 6.0 fusion.62
  36.9 6.0 fusion.62
  64.9 6.0 fusion.62
  92.9 6.0 fusion.62
  120.8 6.0 fusion.62
  148.8 6.0 fusion.62
  176.8 6.0 fusion.62
  204.8 6.0 fusion.62
  232.8 6.0 fusion.62
  260.8 6.0 fusion.62
  288.8 6.0 fusion.62
  316.8 6.0 fusion.62
  344.8 6.0 fusion.62
  372.8 6.0 fusion.62
  400.7 6.0 fusion.62
  428.7 6.0 fusion.62
  456.7 6.0 fusion.62
  484.7 6.0 fusion.62
  512.7 6.0 fusion.62
  540.7 6.0 fusion.62
  568.7 6.0 fusion.62
  596.7 6.0 fusion.62
  624.7 6.0 fusion.62
  (764 shorter events, 504.3 us)
Async XLA Ops:
  14.9 7.3 %all-to-all-start = ((bf16[4,8,768]{2,1,0:T(8,128)(2,1)}), bf16[4,8,768]{2,1,0:T(8,128)(2,1)S(1)}, u32[]{:S(2)}, u32[]{:S(2)}) async-start(bf16[4,8,768]{2,1,0:T(8,128)(2,1)} %fusion.62), calls=%async_computation | async-start | bytes 98304 | tf_op jit(solution)/shard_map/while/body/eval_jaxpr/all_to_all | solution.py:52
  42.9 7.3 %all-to-all-start = ((bf16[4,8,768]{2,1,0:T(8,128)(2,1)}), bf16[4,8,768]{2,1,0:T(8,128)(2,1)S(1)}, u32[]{:S(2)}, u32[]{:S(2)}) async-start(bf16[4,8,768]{2,1,0:T(8,128)(2,1)} %fusion.62), calls=%async_computation | async-start | bytes 98304 | tf_op jit(solution)/shard_map/while/body/eval_jaxpr/all_to_all | solution.py:52
  70.9 7.3 %all-to-all-start = ((bf16[4,8,768]{2,1,0:T(8,128)(2,1)}), bf16[4,8,768]{2,1,0:T(8,128)(2,1)S(1)}, u32[]{:S(2)}, u32[]{:S(2)}) async-start(bf16[4,8,768]{2,1,0:T(8,128)(2,1)} %fusion.62), calls=%async_computation | async-start | bytes 98304 | tf_op jit(solution)/shard_map/while/body/eval_jaxpr/all_to_all | solution.py:52
  98.9 7.3 %all-to-all-start = ((bf16[4,8,768]{2,1,0:T(8,128)(2,1)}), bf16[4,8,768]{2,1,0:T(8,128)(2,1)S(1)}, u32[]{:S(2)}, u32[]{:S(2)}) async-start(bf16[4,8,768]{2,1,0:T(8,128)(2,1)} %fusion.62), calls=%async_computation | async-start | bytes 98304 | tf_op jit(solution)/shard_map/while/body/eval_jaxpr/all_to_all | solution.py:52
  126.9 7.3 %all-to-all-start = ((bf16[4,8,768]{2,1,0:T(8,128)(2,1)}), bf16[4,8,768]{2,1,0:T(8,128)(2,1)S(1)}, u32[]{:S(2)}, u32[]{:S(2)}) async-start(bf16[4,8,768]{2,1,0:T(8,128)(2,1)} %fusion.62), calls=%async_computation | async-start | bytes 98304 | tf_op jit(solution)/shard_map/while/body/eval_jaxpr/all_to_all | solution.py:52
  154.9 7.3 %all-to-all-start = ((bf16[4,8,768]{2,1,0:T(8,128)(2,1)}), bf16[4,8,768]{2,1,0:T(8,128)(2,1)S(1)}, u32[]{:S(2)}, u32[]{:S(2)}) async-start(bf16[4,8,768]{2,1,0:T(8,128)(2,1)} %fusion.62), calls=%async_computation | async-start | bytes 98304 | tf_op jit(solution)/shard_map/while/body/eval_jaxpr/all_to_all | solution.py:52
  182.9 7.3 %all-to-all-start = ((bf16[4,8,768]{2,1,0:T(8,128)(2,1)}), bf16[4,8,768]{2,1,0:T(8,128)(2,1)S(1)}, u32[]{:S(2)}, u32[]{:S(2)}) async-start(bf16[4,8,768]{2,1,0:T(8,128)(2,1)} %fusion.62), calls=%async_computation | async-start | bytes 98304 | tf_op jit(solution)/shard_map/while/body/eval_jaxpr/all_to_all | solution.py:52
  210.9 7.3 %all-to-all-start = ((bf16[4,8,768]{2,1,0:T(8,128)(2,1)}), bf16[4,8,768]{2,1,0:T(8,128)(2,1)S(1)}, u32[]{:S(2)}, u32[]{:S(2)}) async-start(bf16[4,8,768]{2,1,0:T(8,128)(2,1)} %fusion.62), calls=%async_computation | async-start | bytes 98304 | tf_op jit(solution)/shard_map/while/body/eval_jaxpr/all_to_all | solution.py:52
  238.8 7.3 %all-to-all-start = ((bf16[4,8,768]{2,1,0:T(8,128)(2,1)}), bf16[4,8,768]{2,1,0:T(8,128)(2,1)S(1)}, u32[]{:S(2)}, u32[]{:S(2)}) async-start(bf16[4,8,768]{2,1,0:T(8,128)(2,1)} %fusion.62), calls=%async_computation | async-start | bytes 98304 | tf_op jit(solution)/shard_map/while/body/eval_jaxpr/all_to_all | solution.py:52
  266.8 7.3 %all-to-all-start = ((bf16[4,8,768]{2,1,0:T(8,128)(2,1)}), bf16[4,8,768]{2,1,0:T(8,128)(2,1)S(1)}, u32[]{:S(2)}, u32[]{:S(2)}) async-start(bf16[4,8,768]{2,1,0:T(8,128)(2,1)} %fusion.62), calls=%async_computation | async-start | bytes 98304 | tf_op jit(solution)/shard_map/while/body/eval_jaxpr/all_to_all | solution.py:52
  294.8 7.3 %all-to-all-start = ((bf16[4,8,768]{2,1,0:T(8,128)(2,1)}), bf16[4,8,768]{2,1,0:T(8,128)(2,1)S(1)}, u32[]{:S(2)}, u32[]{:S(2)}) async-start(bf16[4,8,768]{2,1,0:T(8,128)(2,1)} %fusion.62), calls=%async_computation | async-start | bytes 98304 | tf_op jit(solution)/shard_map/while/body/eval_jaxpr/all_to_all | solution.py:52
  322.8 7.3 %all-to-all-start = ((bf16[4,8,768]{2,1,0:T(8,128)(2,1)}), bf16[4,8,768]{2,1,0:T(8,128)(2,1)S(1)}, u32[]{:S(2)}, u32[]{:S(2)}) async-start(bf16[4,8,768]{2,1,0:T(8,128)(2,1)} %fusion.62), calls=%async_computation | async-start | bytes 98304 | tf_op jit(solution)/shard_map/while/body/eval_jaxpr/all_to_all | solution.py:52
  350.8 7.3 %all-to-all-start = ((bf16[4,8,768]{2,1,0:T(8,128)(2,1)}), bf16[4,8,768]{2,1,0:T(8,128)(2,1)S(1)}, u32[]{:S(2)}, u32[]{:S(2)}) async-start(bf16[4,8,768]{2,1,0:T(8,128)(2,1)} %fusion.62), calls=%async_computation | async-start | bytes 98304 | tf_op jit(solution)/shard_map/while/body/eval_jaxpr/all_to_all | solution.py:52
  378.8 7.3 %all-to-all-start = ((bf16[4,8,768]{2,1,0:T(8,128)(2,1)}), bf16[4,8,768]{2,1,0:T(8,128)(2,1)S(1)}, u32[]{:S(2)}, u32[]{:S(2)}) async-start(bf16[4,8,768]{2,1,0:T(8,128)(2,1)} %fusion.62), calls=%async_computation | async-start | bytes 98304 | tf_op jit(solution)/shard_map/while/body/eval_jaxpr/all_to_all | solution.py:52
  406.8 7.3 %all-to-all-start = ((bf16[4,8,768]{2,1,0:T(8,128)(2,1)}), bf16[4,8,768]{2,1,0:T(8,128)(2,1)S(1)}, u32[]{:S(2)}, u32[]{:S(2)}) async-start(bf16[4,8,768]{2,1,0:T(8,128)(2,1)} %fusion.62), calls=%async_computation | async-start | bytes 98304 | tf_op jit(solution)/shard_map/while/body/eval_jaxpr/all_to_all | solution.py:52
  414.3 6.5 %collective-permute-start = (bf16[8,768]{1,0:T(8,128)(2,1)S(1)}, bf16[8,768]{1,0:T(8,128)(2,1)S(1)}, u32[]{:S(2)}, u32[]{:S(2)}) collective-permute-start(bf16[8,768]{1,0:T(8,128)(2,1)S(1)} %get-tuple-element.505), channel_id=1, source_target_pairs={{0,4},{4,8},{8,12},{12,16},{16,20},{20,24},{24,28},{1,5},{5,9},{9,... | collective-permute-start | bytes 36872 | tf_op jit(solution)/shard_map/while/body/eval_jaxpr/ppermute | solution.py:12
  434.8 7.3 %all-to-all-start = ((bf16[4,8,768]{2,1,0:T(8,128)(2,1)}), bf16[4,8,768]{2,1,0:T(8,128)(2,1)S(1)}, u32[]{:S(2)}, u32[]{:S(2)}) async-start(bf16[4,8,768]{2,1,0:T(8,128)(2,1)} %fusion.62), calls=%async_computation | async-start | bytes 98304 | tf_op jit(solution)/shard_map/while/body/eval_jaxpr/all_to_all | solution.py:52
  462.8 7.3 %all-to-all-start = ((bf16[4,8,768]{2,1,0:T(8,128)(2,1)}), bf16[4,8,768]{2,1,0:T(8,128)(2,1)S(1)}, u32[]{:S(2)}, u32[]{:S(2)}) async-start(bf16[4,8,768]{2,1,0:T(8,128)(2,1)} %fusion.62), calls=%async_computation | async-start | bytes 98304 | tf_op jit(solution)/shard_map/while/body/eval_jaxpr/all_to_all | solution.py:52
  490.8 7.3 %all-to-all-start = ((bf16[4,8,768]{2,1,0:T(8,128)(2,1)}), bf16[4,8,768]{2,1,0:T(8,128)(2,1)S(1)}, u32[]{:S(2)}, u32[]{:S(2)}) async-start(bf16[4,8,768]{2,1,0:T(8,128)(2,1)} %fusion.62), calls=%async_computation | async-start | bytes 98304 | tf_op jit(solution)/shard_map/while/body/eval_jaxpr/all_to_all | solution.py:52
  518.7 7.3 %all-to-all-start = ((bf16[4,8,768]{2,1,0:T(8,128)(2,1)}), bf16[4,8,768]{2,1,0:T(8,128)(2,1)S(1)}, u32[]{:S(2)}, u32[]{:S(2)}) async-start(bf16[4,8,768]{2,1,0:T(8,128)(2,1)} %fusion.62), calls=%async_computation | async-start | bytes 98304 | tf_op jit(solution)/shard_map/while/body/eval_jaxpr/all_to_all | solution.py:52
  546.7 7.3 %all-to-all-start = ((bf16[4,8,768]{2,1,0:T(8,128)(2,1)}), bf16[4,8,768]{2,1,0:T(8,128)(2,1)S(1)}, u32[]{:S(2)}, u32[]{:S(2)}) async-start(bf16[4,8,768]{2,1,0:T(8,128)(2,1)} %fusion.62), calls=%async_computation | async-start | bytes 98304 | tf_op jit(solution)/shard_map/while/body/eval_jaxpr/all_to_all | solution.py:52
  574.7 7.3 %all-to-all-start = ((bf16[4,8,768]{2,1,0:T(8,128)(2,1)}), bf16[4,8,768]{2,1,0:T(8,128)(2,1)S(1)}, u32[]{:S(2)}, u32[]{:S(2)}) async-start(bf16[4,8,768]{2,1,0:T(8,128)(2,1)} %fusion.62), calls=%async_computation | async-start | bytes 98304 | tf_op jit(solution)/shard_map/while/body/eval_jaxpr/all_to_all | solution.py:52
  602.7 7.3 %all-to-all-start = ((bf16[4,8,768]{2,1,0:T(8,128)(2,1)}), bf16[4,8,768]{2,1,0:T(8,128)(2,1)S(1)}, u32[]{:S(2)}, u32[]{:S(2)}) async-start(bf16[4,8,768]{2,1,0:T(8,128)(2,1)} %fusion.62), calls=%async_computation | async-start | bytes 98304 | tf_op jit(solution)/shard_map/while/body/eval_jaxpr/all_to_all | solution.py:52
  630.7 7.3 %all-to-all-start = ((bf16[4,8,768]{2,1,0:T(8,128)(2,1)}), bf16[4,8,768]{2,1,0:T(8,128)(2,1)S(1)}, u32[]{:S(2)}, u32[]{:S(2)}) async-start(bf16[4,8,768]{2,1,0:T(8,128)(2,1)} %fusion.62), calls=%async_computation | async-start | bytes 98304 | tf_op jit(solution)/shard_map/while/body/eval_jaxpr/all_to_all | solution.py:52
  (46 other events, 358.0 us)
where the time goes:
time: 651 us; the launch traced here: 645 us
  waiting for transfers between devices  190 us (29%)
  matrix products  150 us (23%)
  starting transfers between devices  121 us (19%)
  blocking collectives  120 us (18%)
  other arithmetic  51.5 us (8%)
  local copies, waits for them, and re-layouts  10.7 us (2%)
    dot_general x23, matrix products, apply_expert(): jnp.dot(hidden, expert_out, preferred_element_type=jnp.float32)  139 us
    all_gather x23, blocking collectives, apply_layer(): lax.all_gather(normed, 'expert', axis=0, tiled=True)  120 us
    ppermute x23, waiting for transfers between devices, from_behind(): return lax.ppermute(block, axis, route)  103 us
    all_to_all x23, waiting for transfers between devices, apply_expert(): lax.all_to_all(produced.reshape(received.shape), 'expert', split_axis=0,...  87.2 us
    all_to_all x23, starting transfers between devices, apply_expert(): lax.all_to_all(produced.reshape(received.shape), 'expert', split_axis=0,...  75.3 us
    ppermute x23, starting transfers between devices, from_behind(): return lax.ppermute(block, axis, route)  46 us
    reduce_sum x23, other arithmetic, apply_layer(): jnp.mean(stream * stream, axis=-1, keepdims=True) + epsilon  19.2 us
    mul x23, other arithmetic, apply_layer(): normed = (stream * inverse * gain_row).astype(jnp.bfloat16)  16.1 us
  transfers between devices with their start and end apart: 46, of which 46 were waited for; matrix products, arithmetic and copies ran while one was open for 1% of the time, Pallas kernels for 0%

commit v1 on v0

--- a/solution.py
+++ b/solution.py
@@ -4,6 +4,19 @@
 from jax.sharding import PartitionSpec as P
 
 epsilon = 1e-06
+
+
+def gather_around(shard, axis, dim):
+    size, index, rows = (lax.axis_size(axis), lax.axis_index(axis), shard.shape[dim])
+    right = [(i, (i + 1) % size) for i in range(size)]
+    out = jnp.zeros((*shard.shape[:dim], size * rows, *shard.shape[dim + 1 :]), shard.dtype)
+    held = shard
+    for turn in range(size):
+        owner = (index - turn) % size
+        out = lax.dynamic_update_slice_in_dim(out, held, owner * rows, axis=dim)
+        if turn < size - 1:
+            held = lax.ppermute(held, axis, right)
+    return out
 
 
 def from_behind(block, axis, distance):
@@ -72,7 +85,7 @@
         picker = picker.reshape(groups * tok_rows, groups * capacity)
         collected = lax.dot_general(
             picker,
-            lax.all_gather(normed, "expert", axis=0, tiled=True),
+            gather_around(normed, "expert", 0),
             contract_rows,
             preferred_element_type=jnp.float32,
         )

time: 651 us -> 728 us (1.12)
  waiting for transfers between devices: 190 us -> 366 us
  blocking collectives: 120 us -> 0 us
  matrix products: 150 us -> 166 us
    ppermute x0 -> x69, waiting for transfers between devices: none -> 172 us  [gather_around(): held = lax.ppermute(held, axis, right)]
    all_gather x23 -> x0, blocking collectives: 120 us -> none  [apply_layer(): lax.all_gather(normed, 'expert', axis=0, tiled=True)]
    dot_general x23, matrix products: 2.74 us -> 18.8 us  [apply_layer(): logits = jnp.dot(normed, router_block, preferred_element_type=jnp.float32)]
  transfers between devices with their start and end apart: 46 -> 115, of which waited for: 46 -> 115; matrix products, arithmetic and copies ran while one was open for 1% -> 6% of each run, Pallas kernels for 0% -> 0%
where the time goes in v1:
time: 728 us; the launch traced here: 721 us
  waiting for transfers between devices  366 us (50%)
  matrix products  166 us (23%)
  starting transfers between devices  122 us (17%)
  other arithmetic  51.3 us (7%)
  local copies, waits for them, and re-layouts  11.3 us (2%)
    ppermute x69, waiting for transfers between devices, gather_around(): held = lax.ppermute(held, axis, right)  172 us
    dot_general x23, matrix products, apply_expert(): jnp.dot(hidden, expert_out, preferred_element_type=jnp.float32)  139 us
    ppermute x23, waiting for transfers between devices, from_behind(): return lax.ppermute(block, axis, route)  103 us
    all_to_all x23, waiting for transfers between devices, apply_expert(): lax.all_to_all(produced.reshape(received.shape), 'expert', split_axis=0,...  91.3 us
    all_to_all x23, starting transfers between devices, apply_expert(): lax.all_to_all(produced.reshape(received.shape), 'expert', split_axis=0,...  75.3 us
    ppermute x23, starting transfers between devices, from_behind(): return lax.ppermute(block, axis, route)  46 us
    reduce_sum x23, other arithmetic, apply_layer(): jnp.mean(stream * stream, axis=-1, keepdims=True) + epsilon  19 us
    dot_general x23, matrix products, apply_layer(): logits = jnp.dot(normed, router_block, preferred_element_type=jnp.float32)  18.8 us
  transfers between devices with their start and end apart: 115, of which 115 were waited for; matrix products, arithmetic and copies ran while one was open for 6% of the time, Pallas kernels for 0%

profile of v1, /device:TPU:24, one launch (start us, length us, event | category | flops | bytes accessed | tf_op | source)
XLA Modules:
  0.0 720.6 jit_solution(15762747977893608392)
XLA Ops:
  0.9 719.0 %while.18 = (s32[]{:T(128)}, bf16[8,768]{1,0:T(8,128)(2,1)S(1)}, bf16[16,8,768]{2,1,0:T(8,128)(2,1)S(1)}, pred[]{:T(512)}, s32[]{:T(128)}, /*index=5*/bf16[16,8,...) while((s32[]{:T(128)}, bf16[8,768]{1,0:T(8,128)(2,1)S(1)}, ...), condition=%wide.region_6.7_spmd.clone, body=%wide.region_0.6_spmd.clone.sunk | while | flops 304748160 | bytes 10441998 | solution.py:124
  12.1 6.0 fusion.61
  43.4 6.0 fusion.61
  74.7 6.0 fusion.61
  105.9 6.0 fusion.61
  137.2 6.0 fusion.61
  168.4 6.0 fusion.61
  199.7 6.0 fusion.61
  231.0 6.0 fusion.61
  262.2 6.0 fusion.61
  293.5 6.0 fusion.61
  324.7 6.0 fusion.61
  356.0 6.0 fusion.61
  387.2 6.0 fusion.61
  418.5 6.0 fusion.61
  449.8 6.0 fusion.61
  481.0 6.0 fusion.61
  512.3 6.0 fusion.61
  543.5 6.0 fusion.61
  574.8 6.0 fusion.61
  606.0 6.0 fusion.61
  637.3 6.0 fusion.61
  668.6 6.0 fusion.61
  699.8 6.0 fusion.61
  (925 shorter events, 577.4 us)
Async XLA Ops:
  18.2 7.3 %all-to-all-start = ((bf16[4,8,768]{2,1,0:T(8,128)(2,1)}), bf16[4,8,768]{2,1,0:T(8,128)(2,1)S(1)}, u32[]{:S(2)}, u32[]{:S(2)}) async-start(bf16[4,8,768]{2,1,0:T(8,128)(2,1)} %fusion.61), calls=%async_computation | async-start | bytes 98304 | tf_op jit(solution)/shard_map/while/body/eval_jaxpr/all_to_all | solution.py:65
  49.4 7.3 %all-to-all-start = ((bf16[4,8,768]{2,1,0:T(8,128)(2,1)}), bf16[4,8,768]{2,1,0:T(8,128)(2,1)S(1)}, u32[]{:S(2)}, u32[]{:S(2)}) async-start(bf16[4,8,768]{2,1,0:T(8,128)(2,1)} %fusion.61), calls=%async_computation | async-start | bytes 98304 | tf_op jit(solution)/shard_map/while/body/eval_jaxpr/all_to_all | solution.py:65
  80.7 7.3 %all-to-all-start = ((bf16[4,8,768]{2,1,0:T(8,128)(2,1)}), bf16[4,8,768]{2,1,0:T(8,128)(2,1)S(1)}, u32[]{:S(2)}, u32[]{:S(2)}) async-start(bf16[4,8,768]{2,1,0:T(8,128)(2,1)} %fusion.61), calls=%async_computation | async-start | bytes 98304 | tf_op jit(solution)/shard_map/while/body/eval_jaxpr/all_to_all | solution.py:65
  112.0 7.3 %all-to-all-start = ((bf16[4,8,768]{2,1,0:T(8,128)(2,1)}), bf16[4,8,768]{2,1,0:T(8,128)(2,1)S(1)}, u32[]{:S(2)}, u32[]{:S(2)}) async-start(bf16[4,8,768]{2,1,0:T(8,128)(2,1)} %fusion.61), calls=%async_computation | async-start | bytes 98304 | tf_op jit(solution)/shard_map/while/body/eval_jaxpr/all_to_all | solution.py:65
  143.2 7.3 %all-to-all-start = ((bf16[4,8,768]{2,1,0:T(8,128)(2,1)}), bf16[4,8,768]{2,1,0:T(8,128)(2,1)S(1)}, u32[]{:S(2)}, u32[]{:S(2)}) async-start(bf16[4,8,768]{2,1,0:T(8,128)(2,1)} %fusion.61), calls=%async_computation | async-start | bytes 98304 | tf_op jit(solution)/shard_map/while/body/eval_jaxpr/all_to_all | solution.py:65
  174.5 7.3 %all-to-all-start = ((bf16[4,8,768]{2,1,0:T(8,128)(2,1)}), bf16[4,8,768]{2,1,0:T(8,128)(2,1)S(1)}, u32[]{:S(2)}, u32[]{:S(2)}) async-start(bf16[4,8,768]{2,1,0:T(8,128)(2,1)} %fusion.61), calls=%async_computation | async-start | bytes 98304 | tf_op jit(solution)/shard_map/while/body/eval_jaxpr/all_to_all | solution.py:65
  205.7 7.3 %all-to-all-start = ((bf16[4,8,768]{2,1,0:T(8,128)(2,1)}), bf16[4,8,768]{2,1,0:T(8,128)(2,1)S(1)}, u32[]{:S(2)}, u32[]{:S(2)}) async-start(bf16[4,8,768]{2,1,0:T(8,128)(2,1)} %fusion.61), calls=%async_computation | async-start | bytes 98304 | tf_op jit(solution)/shard_map/while/body/eval_jaxpr/all_to_all | solution.py:65
  237.0 7.3 %all-to-all-start = ((bf16[4,8,768]{2,1,0:T(8,128)(2,1)}), bf16[4,8,768]{2,1,0:T(8,128)(2,1)S(1)}, u32[]{:S(2)}, u32[]{:S(2)}) async-start(bf16[4,8,768]{2,1,0:T(8,128)(2,1)} %fusion.61), calls=%async_computation | async-start | bytes 98304 | tf_op jit(solution)/shard_map/while/body/eval_jaxpr/all_to_all | solution.py:65
  268.3 7.3 %all-to-all-start = ((bf16[4,8,768]{2,1,0:T(8,128)(2,1)}), bf16[4,8,768]{2,1,0:T(8,128)(2,1)S(1)}, u32[]{:S(2)}, u32[]{:S(2)}) async-start(bf16[4,8,768]{2,1,0:T(8,128)(2,1)} %fusion.61), calls=%async_computation | async-start | bytes 98304 | tf_op jit(solution)/shard_map/while/body/eval_jaxpr/all_to_all | solution.py:65
  299.5 7.3 %all-to-all-start = ((bf16[4,8,768]{2,1,0:T(8,128)(2,1)}), bf16[4,8,768]{2,1,0:T(8,128)(2,1)S(1)}, u32[]{:S(2)}, u32[]{:S(2)}) async-start(bf16[4,8,768]{2,1,0:T(8,128)(2,1)} %fusion.61), calls=%async_computation | async-start | bytes 98304 | tf_op jit(solution)/shard_map/while/body/eval_jaxpr/all_to_all | solution.py:65
  330.8 7.3 %all-to-all-start = ((bf16[4,8,768]{2,1,0:T(8,128)(2,1)}), bf16[4,8,768]{2,1,0:T(8,128)(2,1)S(1)}, u32[]{:S(2)}, u32[]{:S(2)}) async-start(bf16[4,8,768]{2,1,0:T(8,128)(2,1)} %fusion.61), calls=%async_computation | async-start | bytes 98304 | tf_op jit(solution)/shard_map/while/body/eval_jaxpr/all_to_all | solution.py:65
  362.0 7.3 %all-to-all-start = ((bf16[4,8,768]{2,1,0:T(8,128)(2,1)}), bf16[4,8,768]{2,1,0:T(8,128)(2,1)S(1)}, u32[]{:S(2)}, u32[]{:S(2)}) async-start(bf16[4,8,768]{2,1,0:T(8,128)(2,1)} %fusion.61), calls=%async_computation | async-start | bytes 98304 | tf_op jit(solution)/shard_map/while/body/eval_jaxpr/all_to_all | solution.py:65
  369.6 6.5 collective-permute-start.3
  393.3 7.3 %all-to-all-start = ((bf16[4,8,768]{2,1,0:T(8,128)(2,1)}), bf16[4,8,768]{2,1,0:T(8,128)(2,1)S(1)}, u32[]{:S(2)}, u32[]{:S(2)}) async-start(bf16[4,8,768]{2,1,0:T(8,128)(2,1)} %fusion.61), calls=%async_computation | async-start | bytes 98304 | tf_op jit(solution)/shard_map/while/body/eval_jaxpr/all_to_all | solution.py:65
  424.5 7.3 %all-to-all-start = ((bf16[4,8,768]{2,1,0:T(8,128)(2,1)}), bf16[4,8,768]{2,1,0:T(8,128)(2,1)S(1)}, u32[]{:S(2)}, u32[]{:S(2)}) async-start(bf16[4,8,768]{2,1,0:T(8,128)(2,1)} %fusion.61), calls=%async_computation | async-start | bytes 98304 | tf_op jit(solution)/shard_map/while/body/eval_jaxpr/all_to_all | solution.py:65
  455.8 7.3 %all-to-all-start = ((bf16[4,8,768]{2,1,0:T(8,128)(2,1)}), bf16[4,8,768]{2,1,0:T(8,128)(2,1)S(1)}, u32[]{:S(2)}, u32[]{:S(2)}) async-start(bf16[4,8,768]{2,1,0:T(8,128)(2,1)} %fusion.61), calls=%async_computation | async-start | bytes 98304 | tf_op jit(solution)/shard_map/while/body/eval_jaxpr/all_to_all | solution.py:65
  487.1 7.3 %all-to-all-start = ((bf16[4,8,768]{2,1,0:T(8,128)(2,1)}), bf16[4,8,768]{2,1,0:T(8,128)(2,1)S(1)}, u32[]{:S(2)}, u32[]{:S(2)}) async-start(bf16[4,8,768]{2,1,0:T(8,128)(2,1)} %fusion.61), calls=%async_computation | async-start | bytes 98304 | tf_op jit(solution)/shard_map/while/body/eval_jaxpr/all_to_all | solution.py:65
  518.3 7.3 %all-to-all-start = ((bf16[4,8,768]{2,1,0:T(8,128)(2,1)}), bf16[4,8,768]{2,1,0:T(8,128)(2,1)S(1)}, u32[]{:S(2)}, u32[]{:S(2)}) async-start(bf16[4,8,768]{2,1,0:T(8,128)(2,1)} %fusion.61), calls=%async_computation | async-start | bytes 98304 | tf_op jit(solution)/shard_map/while/body/eval_jaxpr/all_to_all | solution.py:65
  549.6 7.3 %all-to-all-start = ((bf16[4,8,768]{2,1,0:T(8,128)(2,1)}), bf16[4,8,768]{2,1,0:T(8,128)(2,1)S(1)}, u32[]{:S(2)}, u32[]{:S(2)}) async-start(bf16[4,8,768]{2,1,0:T(8,128)(2,1)} %fusion.61), calls=%async_computation | async-start | bytes 98304 | tf_op jit(solution)/shard_map/while/body/eval_jaxpr/all_to_all | solution.py:65
  580.8 7.3 %all-to-all-start = ((bf16[4,8,768]{2,1,0:T(8,128)(2,1)}), bf16[4,8,768]{2,1,0:T(8,128)(2,1)S(1)}, u32[]{:S(2)}, u32[]{:S(2)}) async-start(bf16[4,8,768]{2,1,0:T(8,128)(2,1)} %fusion.61), calls=%async_computation | async-start | bytes 98304 | tf_op jit(solution)/shard_map/while/body/eval_jaxpr/all_to_all | solution.py:65
  612.1 7.3 %all-to-all-start = ((bf16[4,8,768]{2,1,0:T(8,128)(2,1)}), bf16[4,8,768]{2,1,0:T(8,128)(2,1)S(1)}, u32[]{:S(2)}, u32[]{:S(2)}) async-start(bf16[4,8,768]{2,1,0:T(8,128)(2,1)} %fusion.61), calls=%async_computation | async-start | bytes 98304 | tf_op jit(solution)/shard_map/while/body/eval_jaxpr/all_to_all | solution.py:65
  643.3 7.3 %all-to-all-start = ((bf16[4,8,768]{2,1,0:T(8,128)(2,1)}), bf16[4,8,768]{2,1,0:T(8,128)(2,1)S(1)}, u32[]{:S(2)}, u32[]{:S(2)}) async-start(bf16[4,8,768]{2,1,0:T(8,128)(2,1)} %fusion.61), calls=%async_computation | async-start | bytes 98304 | tf_op jit(solution)/shard_map/while/body/eval_jaxpr/all_to_all | solution.py:65
  674.6 7.3 %all-to-all-start = ((bf16[4,8,768]{2,1,0:T(8,128)(2,1)}), bf16[4,8,768]{2,1,0:T(8,128)(2,1)S(1)}, u32[]{:S(2)}, u32[]{:S(2)}) async-start(bf16[4,8,768]{2,1,0:T(8,128)(2,1)} %fusion.61), calls=%async_computation | async-start | bytes 98304 | tf_op jit(solution)/shard_map/while/body/eval_jaxpr/all_to_all | solution.py:65
  705.9 7.3 %all-to-all-start = ((bf16[4,8,768]{2,1,0:T(8,128)(2,1)}), bf16[4,8,768]{2,1,0:T(8,128)(2,1)S(1)}, u32[]{:S(2)}, u32[]{:S(2)}) async-start(bf16[4,8,768]{2,1,0:T(8,128)(2,1)} %fusion.61), calls=%async_computation | async-start | bytes 98304 | tf_op jit(solution)/shard_map/while/body/eval_jaxpr/all_to_all | solution.py:65
  (92 other events, 358.5 us)
